TPU v7x, 256 devices: a whole 4x4x8 slice. The times are simulated.
256 devices in a mesh: dp: 64 (over x, z_lo, y), expert: 4 (over z_hi, core).
Axes of the slice: x: 4, y: 4, z: 8 (z_hi: 2, z_lo: 4; z = z_hi * 4 + z_lo), core: 2. Of those that a mesh axis runs over, the one named last changes fastest.
Arguments:
- master: float32 [4, 7168, 2048], P('expert', 'dp'), may hold values from -6 to 6
- first_moment: float32 [4, 7168, 2048], P('expert', 'dp'), may hold values from -0.06 to 0.06
- second_moment: float32 [4, 7168, 2048], P('expert', 'dp'), may hold values from 1e-05 to 0.001
- rotation: int32 [4, 64, 1], replicated, may hold values from 0 to 63; in each aligned block of 64 rows (0 to 63, 64 to 127, ..., all dimensions but the last counted through in order) at most 3 rows name the same one
- assignment: int32 [256], replicated, may hold values from 0 to 255, each once
Outputs:
- saved_master: float32 [4, 256, 3, 448, 128], P('expert', 'dp')
- saved_update: float32 [4, 256, 3, 448, 128], P('expert', 'dp')
- checksums: float32 [4, 2, 256], replicated
Inputs may be any that keep to these rules, and one draw needn't show every extreme that they name: rotation[r, j, 0] is the dp index that writes span j of round r; within one round no index is named more than 3 times, and in some round one index is named exactly 3 times. `assignment`: a permutation of the spans' checksum slots.
All inputs are finite; a program needn't handle non-finite values.
Results may differ from a plain program's by a relative error of at most 0.00002.
Values sent between devices are 32-bit elements; how exact they have to be, the bound alone decides.
A program may use at most 64 MiB of HBM per device.

v0:
```python
import math
import jax
import jax.numpy as jnp
from jax import lax
from jax.sharding import Mesh
from jax.sharding import PartitionSpec as P

LANE = 128
MOST = 3
STEP = 20
DP = ("dp_0", "dp_1", "dp_2")
EXPERT = ("expert_0", "expert_1")
DP_EXPERT = ("dp_0", "dp_1", "dp_2", "expert_0", "expert_1")
BETA_ONE = 0.9
BETA_TWO = 0.95
EPSILON = 1e-08


def sent_together(arrays, axis, split_dim, concat_dim, along):
    ends, at = ([], 0)
    for a in arrays[:-1]:
        at += a.shape[along]
        ends.append(at)
    both = jnp.concatenate(arrays, axis=along)
    return tuple(
        jnp.split(
            lax.all_to_all(both, axis, split_axis=split_dim, concat_axis=concat_dim, tiled=True),
            ends,
            axis=along,
        )
    )


def one_axis_at_a_time(array, axes):
    for axis in axes:
        array = lax.psum(array, axis)
    return array


def scaled_moment(first_part, second_part):
    corr_one = 1.0 - BETA_ONE**STEP
    corr_two = 1.0 - BETA_TWO**STEP
    return first_part / corr_one / (jnp.sqrt(second_part / corr_two) + EPSILON)


def slot_table(rotation, dp_count, most_slots):
    owners = rotation[:, :, 0]
    span_ids = jnp.arange(dp_count, dtype=jnp.int32)
    same_writer = owners[:, :, None] == owners[:, None, :]
    before = span_ids[None, :] < span_ids[:, None]
    slot_rank = jnp.sum((same_writer & before[None]).astype(jnp.int32), axis=2)
    writers = jnp.arange(dp_count, dtype=jnp.int32)
    slot_ids = jnp.arange(most_slots, dtype=jnp.int32)
    matches = (owners[:, None, None, :] == writers[None, None, :, None]) & (
        slot_rank[:, None, None, :] == slot_ids[None, :, None, None]
    )
    matches = matches.astype(jnp.int32)
    found_any = jnp.sum(matches, axis=3)
    picked = jnp.sum(matches * span_ids, axis=3)
    return picked + (1 - found_any) * dp_count


def position_weights(line_ids, per_row, lane_count):
    row_ids = line_ids // per_row
    col_ids = line_ids % per_row * lane_count
    lane_ids = jnp.arange(lane_count, dtype=jnp.int32)
    pattern = (row_ids[..., None] * 5 + (col_ids[..., None] + lane_ids) * 3) % 11
    return 1.0 + pattern.astype(jnp.float32) / 10.0


def deliver_slots(send_parts):
    return sent_together((send_parts[0], send_parts[1]), DP, 1, 1, 0)


def shards(master, first_moment, second_moment, rotation, assignment):
    dp_count = lax.axis_size(DP)
    group_count = lax.axis_size(EXPERT)
    position = lax.axis_index(DP)
    group_id = lax.axis_index(EXPERT)
    round_count = rotation.shape[0]
    rows_here = master.shape[1]
    lane_count = LANE
    per_row = master.shape[2] // lane_count
    lines_device = rows_here * per_row
    piece_len = lines_device // (round_count * dp_count)
    inv_count = 1.0 / math.sqrt(dp_count * piece_len * lane_count)
    table = slot_table(rotation, dp_count, MOST)
    round_ids = jnp.arange(round_count, dtype=jnp.int32)[:, None, None]

    def line_pieces(field_in):
        return field_in.reshape(round_count, dp_count, piece_len, lane_count)

    def padded_pieces(line_view):
        return jnp.concatenate(
            [line_view, jnp.zeros((round_count, 1, piece_len, lane_count), line_view.dtype)], axis=1
        )

    update = scaled_moment(first_moment, second_moment)
    master_lines = line_pieces(master)
    update_lines = line_pieces(update)
    local_lines = position * lines_device + jnp.arange(lines_device, dtype=jnp.int32).reshape(
        round_count, dp_count, piece_len
    )
    weights = position_weights(local_lines, per_row, lane_count)
    master_sums = (
        jnp.sum(master_lines * weights, axis=(2, 3)).reshape(round_count * dp_count) * inv_count
    )
    update_sums = (
        jnp.sum(update_lines * weights, axis=(2, 3)).reshape(round_count * dp_count) * inv_count
    )
    sources = (padded_pieces(master_lines), padded_pieces(update_lines))
    send_parts = tuple(
        (
            source[round_ids, table].reshape(round_count * MOST, dp_count, piece_len, lane_count)
            for source in sources
        )
    )
    delivered = deliver_slots(send_parts)
    saved_master = delivered[0].reshape(round_count, MOST, dp_count, piece_len, lane_count)
    saved_update = delivered[1].reshape(round_count, MOST, dp_count, piece_len, lane_count)
    span_count = assignment.shape[0]
    slot_ids = jnp.arange(span_count, dtype=jnp.int32)
    permuting = (assignment[:, None] == slot_ids[None, :]).astype(jnp.float32)
    both_sums = jnp.stack([master_sums, update_sums])
    placed_sums = jnp.sum(both_sums[:, :, None] * permuting[None], axis=1)
    in_slot = (jnp.arange(group_count, dtype=jnp.int32) == group_id).astype(jnp.float32)
    contribution = in_slot[:, None, None] * placed_sums[None]
    checksums = one_axis_at_a_time(contribution, DP_EXPERT)
    shape_out = (1, round_count, MOST, dp_count * piece_len, lane_count)
    return (saved_master.reshape(shape_out), saved_update.reshape(shape_out), checksums)


def solution(mesh):
    torus = Mesh(
        mesh.devices.reshape(4, 4, 4, 2, 2), ("dp_0", "dp_1", "dp_2", "expert_0", "expert_1")
    )
    in_specs = (P(EXPERT, DP, None), P(EXPERT, DP, None), P(EXPERT, DP, None), P(), P())
    out_specs = (P(EXPERT, DP, None, None, None), P(EXPERT, DP, None, None, None), P())
    return jax.shard_map(
        shards, mesh=torus, in_specs=in_specs, out_specs=out_specs, check_vma=False
    )
```

profile of v0, /device:TPU:71, one launch (start us, length us, event | category | flops | bytes accessed | tf_op | source)
XLA Modules:
  0.0 217.4 jit_solution(6803758860566984017)
XLA Ops:
  0.7 0.8 iota_compare_fusion.1
  1.4 1.0 convert_reduce_fusion
  2.4 0.5 fusion.7
  3.0 0.1 reshape.229
  3.1 1.8 add_divide_fusion
  4.9 0.2 reshape.221
  5.1 1.2 reshape.219
  6.3 0.1 concatenate.15
  6.3 1.3 concatenate.13
  7.6 6.6 %gather_fusion = f32[768,7,128]{2,1,0:T(8,128)} fusion(f32[4,65,7,128]{3,2,1,0:T(8,128)S(1)} %concatenate.13, s32[768]{0:T(1024)S(1)} %reshape.229), kind=kCustom, calls=%fused_computation | custom fusion | bytes 5511168 | tf_op jit(solution)/shard_map/gather | solution.py:114
  14.3 5.3 %copy.16 = f32[12,64,7,128]{3,0,2,1:T(8,128)} copy(f32[12,64,7,128]{3,2,1,0:T(8,128)} %bitcast.12) | data formatting | bytes 5505024 | tf_op jit(solution)/shard_map/reshape | solution.py:114
  19.6 6.6 %gather_fusion.1 = f32[768,7,128]{2,1,0:T(8,128)} fusion(f32[4,65,7,128]{3,2,1,0:T(8,128)S(1)} %concatenate.15, s32[768]{0:T(1024)S(1)} %reshape.229), kind=kCustom, calls=%fused_computation.1 | custom fusion | bytes 5511168 | tf_op jit(solution)/shard_map/gather | solution.py:114
  26.2 3.7 %copy.17 = f32[12,64,7,128]{3,0,2,1:T(8,128)S(1)} copy(f32[12,64,7,128]{3,2,1,0:T(8,128)} %bitcast.11) | data formatting | bytes 5505024 | tf_op jit(solution)/shard_map/reshape | solution.py:114
  29.9 3.0 %pad_maximum_fusion = f32[24,64,7,128]{3,0,2,1:T(8,128)} fusion(f32[12,64,7,128]{3,0,2,1:T(8,128)S(1)} %copy.17, f32[12,64,7,128]{3,0,2,1:T(8,128)S(1)} %copy-done), kind=kLoop, calls=%fused_computation.2 | loop fusion | flops 1376256 | bytes 11010048 | tf_op jit(solution)/shard_map/concatenate | solution.py:24
  32.9 11.1 %all-to-all-start = ((f32[24,64,7,128]{3,0,2,1:T(8,128)}), f32[24,64,7,128]{3,0,2,1:T(8,128)}, u32[]{:S(2)}, u32[]{:S(2)}) async-start(f32[24,64,7,128]{3,0,2,1:T(8,128)} %pad_maximum_fusion), calls=%async_computation | async-start | bytes 11010048 | tf_op jit(solution)/shard_map/all_to_all | solution.py:27
  44.1 0.1 fusion.9
  44.2 7.0 %multiply_reduce_fusion.1 = (f32[4,64]{1,0:T(4,128)S(1)}, f32[4,64]{1,0:T(4,128)S(1)}) fusion(f32[4,64,7,128]{3,2,1,0:T(8,128)S(1)} %copy-done.1, s32[4,64,7]{2,1,0:T(8,128)S(1)} %get-tuple-element.10, s32[4,64,7]{2,1,0:T(8,128)S(1)} %get-tuple-element.9, f32[4,64,7,128]{3,2,1,0:T(8,128)S(1)} %reshape.221), kind=kLoop, calls=%fused_computation.8 | loop fusion | flops 3669504 | bytes 1851392 | tf_op jit(solution)/shard_map/reduce_sum | solution.py:106
  51.2 0.1 mul.152
  51.3 0.1 mul.155
  51.4 0.1 fusion.8
  51.5 0.1 multiply_reduce_fusion.2
  51.7 0.1 broadcast_multiply_fusion
  51.7 21.1 %psum.35 = f32[4,2,256]{2,1,0:T(2,128)S(1)} all-reduce(f32[4,2,256]{2,1,0:T(2,128)S(1)} %broadcast_multiply_fusion), channel_id=1, replica_groups=mesh['dp_0'=4,'dp_1'=4,'dp_2'=4,'expert_0'=2,'expert_1'=2] {'dp_0'}, use_global_device_ids=true, to_apply=%region_6.7 | all-reduce | flops 2048 | bytes 16384 | tf_op jit(solution)/shard_map/psum | solution.py:36
  72.9 92.0 %psum.36 = f32[4,2,256]{2,1,0:T(2,128)S(1)} all-reduce(f32[4,2,256]{2,1,0:T(2,128)S(1)} %psum.35), channel_id=1, replica_groups=mesh['dp_0'=4,'dp_1'=4,'dp_2'=4,'expert_0'=2,'expert_1'=2] {'dp_1'}, use_global_device_ids=true, to_apply=%region_7.8 | all-reduce | flops 2048 | bytes 16384 | tf_op jit(solution)/shard_map/psum | solution.py:36
  164.9 8.5 %psum.37 = f32[4,2,256]{2,1,0:T(2,128)S(1)} all-reduce(f32[4,2,256]{2,1,0:T(2,128)S(1)} %psum.36), channel_id=1, replica_groups=mesh['dp_0'=4,'dp_1'=4,'dp_2'=4,'expert_0'=2,'expert_1'=2] {'dp_2'}, use_global_device_ids=true, to_apply=%region_8.9 | all-reduce | flops 2048 | bytes 16384 | tf_op jit(solution)/shard_map/psum | solution.py:36
  173.4 7.8 %psum.38 = f32[4,2,256]{2,1,0:T(2,128)S(1)} all-reduce(f32[4,2,256]{2,1,0:T(2,128)S(1)} %psum.37), channel_id=1, replica_groups=mesh['dp_0'=4,'dp_1'=4,'dp_2'=4,'expert_0'=2,'expert_1'=2] {'expert_0'}, use_global_device_ids=true, to_apply=%region_9.10 | all-reduce | flops 2048 | bytes 16384 | tf_op jit(solution)/shard_map/psum | solution.py:36
  181.2 8.5 %psum.39 = f32[4,2,256]{2,1,0:T(2,128)} all-reduce(f32[4,2,256]{2,1,0:T(2,128)S(1)} %psum.38), channel_id=1, replica_groups=mesh['dp_0'=4,'dp_1'=4,'dp_2'=4,'expert_0'=2,'expert_1'=2] {'expert_1'}, use_global_device_ids=true, to_apply=%region_10.11 | all-reduce | flops 2048 | bytes 16384 | tf_op jit(solution)/shard_map/psum | solution.py:36
  189.7 6.8 %fusion.17 = (f32[12,64,7,128]{3,0,2,1:T(8,128)}, f32[12,64,7,128]{3,0,2,1:T(8,128)}) fusion(f32[24,64,7,128]{3,0,2,1:T(8,128)} %all-to-all-done), kind=kLoop, calls=%fused_computation.47 | loop fusion | bytes 11010048 | tf_op jit(solution)/shard_map/split | solution.py:26
  196.5 6.0 %reshape.244 = f32[1,4,3,448,128]{4,2,1,3,0:T(4,128)} reshape(f32[12,64,7,128]{3,0,2,1:T(8,128)} %get-tuple-element.7) | data formatting | bytes 5505024 | tf_op jit(solution)/shard_map/reshape;reshape | solution.py:130
  202.5 4.5 %copy.21 = f32[1,4,3,448,128]{4,3,2,1,0:T(8,128)} copy(f32[1,4,3,448,128]{4,2,1,3,0:T(4,128)} %reshape.244) | data formatting | bytes 5505024 | tf_op jit(solution)/shard_map/reshape;reshape | solution.py:130
  206.9 6.0 %reshape.243 = f32[1,4,3,448,128]{4,2,1,3,0:T(4,128)} reshape(f32[12,64,7,128]{3,0,2,1:T(8,128)} %get-tuple-element.8) | data formatting | bytes 5505024 | tf_op jit(solution)/shard_map/reshape;reshape | solution.py:130
  213.0 4.5 %copy.20 = f32[1,4,3,448,128]{4,3,2,1,0:T(8,128)} copy(f32[1,4,3,448,128]{4,2,1,3,0:T(4,128)} %reshape.243) | data formatting | bytes 5505024 | tf_op jit(solution)/shard_map/reshape;reshape | solution.py:130
  (18 shorter events, 0.1 us)
Async XLA Ops:
  0.6 4.5 %copy-start.2 = (f32[1,112,2048]{2,1,0:T(8,128)S(1)}, f32[1,112,2048]{2,1,0:T(8,128)}, u32[]{:S(2)}) copy-start(f32[1,112,2048]{2,1,0:T(8,128)} %param.5) | copy-start | bytes 2752516
  26.2 3.7 %copy-start = (f32[12,64,7,128]{3,0,2,1:T(8,128)S(1)}, f32[12,64,7,128]{3,0,2,1:T(8,128)}, u32[]{:S(2)}) copy-start(f32[12,64,7,128]{3,0,2,1:T(8,128)} %copy.16) | copy-start | bytes 8257540
  32.9 11.3 %copy-start.1 = (f32[4,64,7,128]{3,2,1,0:T(8,128)S(1)}, f32[4,64,7,128]{3,2,1,0:T(8,128)}, u32[]{:S(2)}) copy-start(f32[4,64,7,128]{3,2,1,0:T(8,128)} %reshape.219) | copy-start | bytes 2752516
  32.9 18.5 %copy-start.3 = (s32[256]{0:T(256)S(1)}, s32[256]{0:T(256)}, u32[]{:S(2)}) copy-start(s32[256]{0:T(256)} %param.9) | copy-start | bytes 3076
  32.9 156.7 %all-to-all-start = ((f32[24,64,7,128]{3,0,2,1:T(8,128)}), f32[24,64,7,128]{3,0,2,1:T(8,128)}, u32[]{:S(2)}, u32[]{:S(2)}) async-start(f32[24,64,7,128]{3,0,2,1:T(8,128)} %pad_maximum_fusion), calls=%async_computation | async-start | bytes 11010048 | tf_op jit(solution)/shard_map/all_to_all | solution.py:27
where the time goes:
time: 218 us; the launch traced here: 217 us
  blocking collectives  138 us (63%)
  local copies, waits for them, and re-layouts  53 us (24%)
  other arithmetic  14.6 us (7%)
  starting transfers between devices  11.1 us (5%)
    psum x5, blocking collectives, one_axis_at_a_time(): array = lax.psum(array, axis)  138 us
    gather x2, local copies, waits for them, and re-layouts, shards(): source[round_ids, table]  13.2 us
    all_to_all x1, starting transfers between devices, sent_together(): lax.all_to_all(both, axis, split_axis=split_dim, concat_axis=concat_dim,...  11.1 us
    another operation x2, local copies, waits for them, and re-layouts, shards(): saved_update.reshape(shape_out)  10.5 us
    another operation x2, local copies, waits for them, and re-layouts, shards(): saved_master.reshape(shape_out)  10.5 us
    reshape x2, local copies, waits for them, and re-layouts, shards(): source[round_ids, table]  9.03 us
    reduce_sum x1, other arithmetic, shards(): jnp.sum(master_lines * weights, axis=(2, 3)).reshape(round_count * dp_count)  6.96 us
    split x1, local copies, waits for them, and re-layouts, sent_together(): jnp.split(lax.all_to_all(both, axis, split_axis=split_dim, concat_axis=co...  6.82 us
  transfers between devices with their start and end apart: 1, of which 0 were waited for; matrix products, arithmetic and copies ran while one was open for 3% of the time, Pallas kernels for 0%

commit v1 on v0

--- a/solution.py
+++ b/solution.py
@@ -4,6 +4,7 @@
 from jax import lax
 from jax.sharding import Mesh
 from jax.sharding import PartitionSpec as P
+from jax.lax import all_gather
 
 LANE = 128
 MOST = 3
@@ -33,7 +34,7 @@
 
 def one_axis_at_a_time(array, axes):
     for axis in axes:
-        array = lax.psum(array, axis)
+        array = jnp.sum(all_gather(array, axis), 0)
     return array
 
 

time: 218 us -> 225 us (1.032); the launches traced: 217 us -> 221 us
  blocking collectives: 138 us -> 141 us
    all_gather x0 -> x5, blocking collectives: none -> 141 us  [one_axis_at_a_time(): array = jnp.sum(all_gather(array, axis), 0)]
    psum x5 -> x0, blocking collectives: 138 us -> none  [one_axis_at_a_time(): array = lax.psum(array, axis)]
  transfers between devices with their start and end apart: 1 -> 1, of which waited for: 0 -> 0; matrix products, arithmetic and copies ran while one was open for 3% -> 4% of each run, Pallas kernels for 0% -> 0%
where the time goes in v1:
time: 225 us; the launch traced here: 221 us
  blocking collectives  141 us (63%)
  local copies, waits for them, and re-layouts  53 us (24%)
  other arithmetic  15.3 us (7%)
  starting transfers between devices  11.1 us (5%)
    all_gather x5, blocking collectives, one_axis_at_a_time(): array = jnp.sum(all_gather(array, axis), 0)  141 us
    gather x2, local copies, waits for them, and re-layouts, shards(): source[round_ids, table]  13.2 us
    all_to_all x1, starting transfers between devices, sent_together(): lax.all_to_all(both, axis, split_axis=split_dim, concat_axis=concat_dim,...  11.1 us
    another operation x2, local copies, waits for them, and re-layouts, shards(): saved_update.reshape(shape_out)  10.5 us
    another operation x2, local copies, waits for them, and re-layouts, shards(): saved_master.reshape(shape_out)  10.5 us
    reshape x2, local copies, waits for them, and re-layouts, shards(): source[round_ids, table]  9.03 us
    reduce_sum x1, other arithmetic, shards(): jnp.sum(master_lines * weights, axis=(2, 3)).reshape(round_count * dp_count)  6.96 us
    split x1, local copies, waits for them, and re-layouts, sent_together(): jnp.split(lax.all_to_all(both, axis, split_axis=split_dim, concat_axis=co...  6.82 us
  transfers between devices with their start and end apart: 1, of which 0 were waited for; matrix products, arithmetic and copies ran while one was open for 4% of the time, Pallas kernels for 0%

profile of v1, /device:TPU:71, one launch (start us, length us, event | category | flops | bytes accessed | tf_op | source)
XLA Modules:
  0.0 220.8 jit_solution(14728814399680507617)
XLA Ops:
  0.7 0.8 iota_compare_fusion.1
  1.4 1.0 convert_reduce_fusion
  2.4 0.5 fusion.7
  3.0 0.1 reshape.232
  3.1 1.8 add_divide_fusion
  4.9 0.2 reshape.224
  5.1 1.2 reshape.222
  6.3 1.3 concatenate.13
  7.6 6.6 %gather_fusion = f32[768,7,128]{2,1,0:T(8,128)} fusion(f32[4,65,7,128]{3,2,1,0:T(8,128)S(1)} %concatenate.13, s32[768]{0:T(1024)S(1)} %reshape.232), kind=kCustom, calls=%fused_computation | custom fusion | bytes 5511168 | tf_op jit(solution)/shard_map/gather | solution.py:115
  14.3 5.3 %copy.22 = f32[12,64,7,128]{3,0,2,1:T(8,128)} copy(f32[12,64,7,128]{3,2,1,0:T(8,128)} %bitcast.16) | data formatting | bytes 5505024 | tf_op jit(solution)/shard_map/reshape | solution.py:115
  19.6 6.6 %gather_fusion.1 = f32[768,7,128]{2,1,0:T(8,128)} fusion(f32[4,65,7,128]{3,2,1,0:T(8,128)S(1)} %concatenate.15, s32[768]{0:T(1024)S(1)} %reshape.232), kind=kCustom, calls=%fused_computation.1 | custom fusion | bytes 5511168 | tf_op jit(solution)/shard_map/gather | solution.py:115
  26.2 3.7 %copy.23 = f32[12,64,7,128]{3,0,2,1:T(8,128)S(1)} copy(f32[12,64,7,128]{3,2,1,0:T(8,128)} %bitcast.15) | data formatting | bytes 5505024 | tf_op jit(solution)/shard_map/reshape | solution.py:115
  29.9 3.0 %pad_maximum_fusion = f32[24,64,7,128]{3,0,2,1:T(8,128)} fusion(f32[12,64,7,128]{3,0,2,1:T(8,128)S(1)} %copy.23, f32[12,64,7,128]{3,0,2,1:T(8,128)S(1)} %copy-done), kind=kLoop, calls=%fused_computation.2 | loop fusion | flops 1376256 | bytes 11010048 | tf_op jit(solution)/shard_map/concatenate | solution.py:25
  32.9 11.1 %all-to-all-start = ((f32[24,64,7,128]{3,0,2,1:T(8,128)}), f32[24,64,7,128]{3,0,2,1:T(8,128)}, u32[]{:S(2)}, u32[]{:S(2)}) async-start(f32[24,64,7,128]{3,0,2,1:T(8,128)} %pad_maximum_fusion), calls=%async_computation | async-start | bytes 11010048 | tf_op jit(solution)/shard_map/all_to_all | solution.py:28
  44.1 0.1 fusion.9
  44.2 7.0 %multiply_reduce_fusion.1 = (f32[4,64]{1,0:T(4,128)S(1)}, f32[4,64]{1,0:T(4,128)S(1)}) fusion(f32[4,64,7,128]{3,2,1,0:T(8,128)S(1)} %copy-done.1, s32[4,64,7]{2,1,0:T(8,128)S(1)} %get-tuple-element.10, s32[4,64,7]{2,1,0:T(8,128)S(1)} %get-tuple-element.9, f32[4,64,7,128]{3,2,1,0:T(8,128)S(1)} %reshape.224), kind=kLoop, calls=%fused_computation.8 | loop fusion | flops 3669504 | bytes 1851392 | tf_op jit(solution)/shard_map/reduce_sum | solution.py:107
  51.2 0.1 mul.159
  51.3 0.1 mul.162
  51.4 0.1 fusion.8
  51.5 0.1 multiply_reduce_fusion.2
  51.7 0.1 broadcast_multiply_fusion
  51.7 22.0 %all_gather.28 = f32[4,4,2,256]{3,1,2,0:T(4,128)S(1)} all-gather(f32[1,4,2,256]{3,1,2,0:T(4,128)S(1)} %broadcast_multiply_fusion), channel_id=1, replica_groups=mesh['dp_0'=4,'dp_1'=4,'dp_2'=4,'expert_0'=2,'expert_1'=2] {'dp_0'}, dimensions={0}, use_global_device_ids=true | all-gather | bytes 40960 | tf_op jit(solution)/shard_map/all_gather | solution.py:37
  73.7 92.1 %all-gather = f32[16,2,256]{2,1,0:T(2,128)S(1)} all-gather(f32[4,2,256]{2,1,0:T(2,128)S(1)} %copy.26), channel_id=2, replica_groups=mesh['dp_0'=4,'dp_1'=4,'dp_2'=4,'expert_0'=2,'expert_1'=2] {'dp_1'}, dimensions={0}, use_global_device_ids=true | all-gather | bytes 40960 | tf_op jit(solution)/shard_map/all_gather | solution.py:37
  165.8 11.5 %all-gather.1 = f32[16,2,256]{2,1,0:T(2,128)S(1)} all-gather(f32[4,2,256]{2,1,0:T(2,128)S(1)} %reduce_sum.106), channel_id=3, replica_groups=mesh['dp_0'=4,'dp_1'=4,'dp_2'=4,'expert_0'=2,'expert_1'=2] {'dp_2'}, dimensions={0}, use_global_device_ids=true | all-gather | bytes 40960 | tf_op jit(solution)/shard_map/all_gather | solution.py:37
  177.4 7.1 %all-gather.2 = f32[8,2,256]{2,1,0:T(2,128)S(1)} all-gather(f32[4,2,256]{2,1,0:T(2,128)S(1)} %reduce_sum.107), channel_id=4, replica_groups=mesh['dp_0'=4,'dp_1'=4,'dp_2'=4,'expert_0'=2,'expert_1'=2] {'expert_0'}, dimensions={0}, use_global_device_ids=true | all-gather | bytes 24576 | tf_op jit(solution)/shard_map/all_gather | solution.py:37
  184.5 7.9 %all-gather.3 = f32[8,2,256]{2,1,0:T(2,128)S(1)} all-gather(f32[4,2,256]{2,1,0:T(2,128)S(1)} %reduce_sum.108), channel_id=5, replica_groups=mesh['dp_0'=4,'dp_1'=4,'dp_2'=4,'expert_0'=2,'expert_1'=2] {'expert_1'}, dimensions={0}, use_global_device_ids=true | all-gather | bytes 24576 | tf_op jit(solution)/shard_map/all_gather | solution.py:37
  192.4 0.6 reduce_sum.109
  193.0 6.8 %fusion.17 = (f32[12,64,7,128]{3,0,2,1:T(8,128)}, f32[12,64,7,128]{3,0,2,1:T(8,128)}) fusion(f32[24,64,7,128]{3,0,2,1:T(8,128)} %all-to-all-done), kind=kLoop, calls=%fused_computation.47 | loop fusion | bytes 11010048 | tf_op jit(solution)/shard_map/split | solution.py:27
  199.8 6.0 %reshape.251 = f32[1,4,3,448,128]{4,2,1,3,0:T(4,128)} reshape(f32[12,64,7,128]{3,0,2,1:T(8,128)} %get-tuple-element.7) | data formatting | bytes 5505024 | tf_op jit(solution)/shard_map/reshape;reshape | solution.py:131
  205.8 4.5 %copy.28 = f32[1,4,3,448,128]{4,3,2,1,0:T(8,128)} copy(f32[1,4,3,448,128]{4,2,1,3,0:T(4,128)} %reshape.251) | data formatting | bytes 5505024 | tf_op jit(solution)/shard_map/reshape;reshape | solution.py:131
  210.3 6.0 %reshape.250 = f32[1,4,3,448,128]{4,2,1,3,0:T(4,128)} reshape(f32[12,64,7,128]{3,0,2,1:T(8,128)} %get-tuple-element.8) | data formatting | bytes 5505024 | tf_op jit(solution)/shard_map/reshape;reshape | solution.py:131
  216.3 4.5 %copy.27 = f32[1,4,3,448,128]{4,3,2,1,0:T(8,128)} copy(f32[1,4,3,448,128]{4,2,1,3,0:T(4,128)} %reshape.250) | data formatting | bytes 5505024 | tf_op jit(solution)/shard_map/reshape;reshape | solution.py:131
  (24 shorter events, 0.2 us)
Async XLA Ops:
  0.6 4.5 %copy-start.2 = (f32[1,112,2048]{2,1,0:T(8,128)S(1)}, f32[1,112,2048]{2,1,0:T(8,128)}, u32[]{:S(2)}) copy-start(f32[1,112,2048]{2,1,0:T(8,128)} %param.5) | copy-start | bytes 2752516
  26.2 3.7 %copy-start = (f32[12,64,7,128]{3,0,2,1:T(8,128)S(1)}, f32[12,64,7,128]{3,0,2,1:T(8,128)}, u32[]{:S(2)}) copy-start(f32[12,64,7,128]{3,0,2,1:T(8,128)} %copy.22) | copy-start | bytes 8257540
  32.9 11.3 %copy-start.1 = (f32[4,64,7,128]{3,2,1,0:T(8,128)S(1)}, f32[4,64,7,128]{3,2,1,0:T(8,128)}, u32[]{:S(2)}) copy-start(f32[4,64,7,128]{3,2,1,0:T(8,128)} %reshape.222) | copy-start | bytes 2752516
  32.9 18.5 %copy-start.3 = (s32[256]{0:T(256)S(1)}, s32[256]{0:T(256)}, u32[]{:S(2)}) copy-start(s32[256]{0:T(256)} %param.9) | copy-start | bytes 3076
  32.9 160.1 %all-to-all-start = ((f32[24,64,7,128]{3,0,2,1:T(8,128)}), f32[24,64,7,128]{3,0,2,1:T(8,128)}, u32[]{:S(2)}, u32[]{:S(2)}) async-start(f32[24,64,7,128]{3,0,2,1:T(8,128)} %pad_maximum_fusion), calls=%async_computation | async-start | bytes 11010048 | tf_op jit(solution)/shard_map/all_to_all | solution.py:28
